TPU v7x, 32 devices: a whole 2x2x4 slice. The times are simulated.
32 devices in a mesh: dp: 16 (over z, x, core), tensor: 2 (over y).
Axes of the slice: x: 2, y: 2, z: 4, core: 2. Of those that a mesh axis runs over, the one named last changes fastest.
Arguments:
- tokens: bfloat16 [63040, 384], P(('dp', 'tensor')), may hold values from -6 to 6
- query_key_value: bfloat16 [384, 3, 384], P('dp', None, 'tensor'), may hold values from -0.3125 to 0.3125
- attention_out: bfloat16 [384, 384], P('tensor', 'dp'), may hold values from -1.25 to 1.25
- first_gain: bfloat16 [384], P('dp'), may hold values from 0.099609375 to 1.8984375
- first_shift: bfloat16 [384], P('dp'), may hold values from -3 to 3
- second_gain: bfloat16 [384], P('dp'), may hold values from 0.099609375 to 1.8984375
- second_shift: bfloat16 [384], P('dp'), may hold values from -3 to 3
- expert_in: bfloat16 [8, 384, 1536], P(None, None, ('dp', 'tensor')), may hold values from -0.3125 to 0.3125
- expert_out: bfloat16 [8, 1536, 384], P(None, ('dp', 'tensor')), may hold values from -0.15625 to 0.15625
- expert_ids: int32 [63040, 2], P('dp'), may hold values from 0 to 7, all different within a row; in each aligned block of 3940 rows (0 to 3939, 3940 to 7879, ...) at most 1232 rows name the same one
- gate_weights: float32 [63040, 2], P('dp'), may hold values from 0.1 to 0.9
- cotangent: bfloat16 [63040, 384], P(('dp', 'tensor')), may hold values from -6 to 6
Outputs:
- output: bfloat16 [63040, 384], P(('dp', 'tensor'))
- grad_tokens: float32 [63040, 384], P(('dp', 'tensor'))
- grad_query_key_value: float32 [384, 3, 384], P('dp', None, 'tensor')
- grad_attention_out: float32 [384, 384], P('tensor', 'dp')
- grad_first_gain: float32 [384], P('dp')
- grad_first_shift: float32 [384], P('dp')
- grad_second_gain: float32 [384], P('dp')
- grad_second_shift: float32 [384], P('dp')
- grad_expert_in: float32 [8, 384, 1536], P(None, None, ('dp', 'tensor'))
- grad_expert_out: float32 [8, 1536, 384], P(None, ('dp', 'tensor'))
Inputs may be any that keep to these rules, and one draw needn't show every extreme that they name: `expert_ids`: each row names 2 different experts; within the rows of one index of dp (aligned blocks of 3940 rows) no expert is named by more than 1232 rows, and in some such block one is named by exactly 1232.
All inputs are finite; a program needn't handle non-finite values.
Results may differ from a plain program's by a relative error of at most 0.015.
Values may be sent and summed in bfloat16 or wider, within the bound.
A program may use at most 192 MiB of HBM per device.

v0:
```python
import jax
import jax.numpy as jnp
from jax import lax
from jax.sharding import PartitionSpec as P

HEAD_DIM = 64
SEQ = 197
IMG_BLOCK = 4
CAP = 1232


EPSILON = 1e-06
INV_ROOT_TAU = 0.3989422804014327
INV_ROOT_TWO = 0.7071067811865476


def normalize(matrix, scaling, offset):
    centre = matrix - jnp.mean(matrix, -1, keepdims=True)
    variance = jnp.mean(centre * centre, -1, keepdims=True)
    inverse = lax.rsqrt(variance + EPSILON)
    scaled = centre * inverse
    return (scaled * scaling.astype(jnp.float32) + offset.astype(jnp.float32), scaled, inverse)


def norm_backward(upstream, scaled, inverse, scaling):
    weighted = upstream * scaling.astype(jnp.float32)
    inner = (
        weighted
        - jnp.mean(weighted, -1, keepdims=True)
        - scaled * jnp.mean(weighted * scaled, -1, keepdims=True)
    )
    return (inverse * inner, jnp.sum(upstream * scaled, 0), jnp.sum(upstream, 0))


def gelu_slope(values):
    return (
        0.5 * (1.0 + lax.erf(values * INV_ROOT_TWO))
        + values * jnp.exp(-0.5 * values * values) * INV_ROOT_TAU
    )


def attend_forward(stacked):
    queries = stacked[:, :, 0]
    key_rows = stacked[:, :, 1]
    values = stacked[:, :, 2]
    scores = jnp.einsum(
        "bqhd,bkhd->bhqk", queries, key_rows, preferred_element_type=jnp.float32
    ) * HEAD_DIM ** (-0.5)
    highest = jnp.max(scores, -1, keepdims=True)
    log_total = highest + jnp.log(jnp.sum(jnp.exp(scores - highest), -1, keepdims=True))
    softened = jnp.exp(scores - log_total).astype(jnp.bfloat16)
    blended = jnp.einsum("bhqk,bkhd->bqhd", softened, values, preferred_element_type=jnp.float32)
    return (blended.astype(jnp.bfloat16), log_total[..., 0])


def attend_backward(members):
    stacked, log_total, upstream = members
    queries = stacked[:, :, 0]
    key_rows = stacked[:, :, 1]
    values = stacked[:, :, 2]
    scale_factor = HEAD_DIM ** (-0.5)
    scores = (
        jnp.einsum("bqhd,bkhd->bhqk", queries, key_rows, preferred_element_type=jnp.float32)
        * scale_factor
    )
    softened = jnp.exp(scores - log_total[..., None])
    rounded = softened.astype(jnp.bfloat16)
    grad_values = jnp.einsum(
        "bhqk,bqhd->bkhd", rounded, upstream, preferred_element_type=jnp.float32
    )
    grad_soft = jnp.einsum("bqhd,bkhd->bhqk", upstream, values, preferred_element_type=jnp.float32)
    grad_scores = (
        softened * (grad_soft - jnp.sum(grad_soft * softened, -1, keepdims=True))
    ).astype(jnp.bfloat16)
    grad_queries = (
        jnp.einsum("bhqk,bkhd->bqhd", grad_scores, key_rows, preferred_element_type=jnp.float32)
        * scale_factor
    )
    grad_keys = (
        jnp.einsum("bhqk,bqhd->bkhd", grad_scores, queries, preferred_element_type=jnp.float32)
        * scale_factor
    )
    return jnp.stack([grad_queries, grad_keys, grad_values], 2).astype(jnp.bfloat16)


def expert_pass(normed, upstream, routes, weights, first_layer, second_layer):
    row_count = normed.shape[0]
    feature_count = normed.shape[1]
    number = first_layer.shape[0]
    flattened = routes.reshape(-1)
    matches = (flattened[:, None] == jnp.arange(number, dtype=jnp.int32)[None, :]).astype(jnp.int32)
    slot_rank = jnp.sum((jnp.cumsum(matches, axis=0) - matches) * matches, axis=1)
    position = flattened * CAP + slot_rank
    owners = (
        jnp.full((number * CAP,), row_count, jnp.int32)
        .at[position]
        .set(jnp.arange(flattened.shape[0], dtype=jnp.int32) // routes.shape[1])
    )
    slot_gates = jnp.zeros((number * CAP,), jnp.float32).at[position].set(weights.reshape(-1))
    zero_row = jnp.zeros((1, feature_count), jnp.bfloat16)
    padded = jnp.concatenate([normed, zero_row], 0)
    padded_cot = jnp.concatenate([upstream, zero_row], 0)

    def per_expert(sums_pair, members):
        out_sum, back_sum = sums_pair
        slot_rows, slot_gate, first_piece, second_piece = members
        loaded = padded[slot_rows]
        grad_slot = (padded_cot[slot_rows].astype(jnp.float32) * slot_gate[:, None]).astype(
            jnp.bfloat16
        )
        before_act = jnp.dot(loaded, first_piece, preferred_element_type=jnp.float32)
        active = jax.nn.gelu(before_act, approximate=False).astype(jnp.bfloat16)
        results = jnp.dot(active, second_piece, preferred_element_type=jnp.float32)
        grad_active = lax.dot_general(
            grad_slot, second_piece, (((1,), (1,)), ((), ())), preferred_element_type=jnp.float32
        )
        grad_before = (grad_active * gelu_slope(before_act)).astype(jnp.bfloat16)
        grad_first = lax.dot_general(
            loaded, grad_before, (((0,), (0,)), ((), ())), preferred_element_type=jnp.float32
        )
        grad_second = lax.dot_general(
            active, grad_slot, (((0,), (0,)), ((), ())), preferred_element_type=jnp.float32
        )
        grad_loaded = lax.dot_general(
            grad_before, first_piece, (((1,), (1,)), ((), ())), preferred_element_type=jnp.float32
        )
        out_sum = out_sum.at[slot_rows].add(results * slot_gate[:, None])
        back_sum = back_sum.at[slot_rows].add(grad_loaded)
        return ((out_sum, back_sum), (grad_first, grad_second))

    zeroed = jnp.zeros((row_count + 1, feature_count), jnp.float32)
    totals, gradients = lax.scan(
        per_expert,
        (zeroed, zeroed),
        (owners.reshape(number, CAP), slot_gates.reshape(number, CAP), first_layer, second_layer),
    )
    return (totals[0][:row_count], totals[1][:row_count], gradients[0], gradients[1])


def on_device(
    tokens,
    query_key_value,
    attention_out,
    first_gain,
    first_shift,
    second_gain,
    second_shift,
    expert_in,
    expert_out,
    expert_ids,
    gate_weights,
    cotangent,
):
    own_rows, features = tokens.shape
    joint, out_matrix, gain_one, offset_one, gain_two, offset_two = (
        lax.all_gather(query_key_value, "dp", axis=0, tiled=True),
        lax.all_gather(attention_out, "dp", axis=1, tiled=True),
        lax.all_gather(first_gain, "dp", axis=0, tiled=True),
        lax.all_gather(first_shift, "dp", axis=0, tiled=True),
        lax.all_gather(second_gain, "dp", axis=0, tiled=True),
        lax.all_gather(second_shift, "dp", axis=0, tiled=True),
    )
    local_width = joint.shape[2]
    local_heads = local_width // HEAD_DIM
    joint_matrix = joint.reshape(features, 3 * local_width)
    inputs = tokens.astype(jnp.float32)
    normed_one, scaled_one, inverse_one = normalize(inputs, gain_one, offset_one)
    rows_one = lax.all_gather(normed_one.astype(jnp.bfloat16), "tensor", axis=0, tiled=True)
    group_rows = rows_one.shape[0]
    block_count = group_rows // (IMG_BLOCK * SEQ)
    packed = jnp.dot(rows_one, joint_matrix, preferred_element_type=jnp.float32).astype(
        jnp.bfloat16
    )
    stacked = packed.reshape(block_count, IMG_BLOCK, SEQ, 3, local_heads, HEAD_DIM)
    blended, log_total = lax.map(attend_forward, stacked)
    blended_rows = blended.reshape(group_rows, local_width)
    branch_one = lax.psum_scatter(
        jnp.dot(blended_rows, out_matrix, preferred_element_type=jnp.float32).astype(jnp.bfloat16),
        "tensor",
        scatter_dimension=0,
        tiled=True,
    ).astype(jnp.float32)
    hidden = inputs + branch_one
    normed_two, scaled_two, inverse_two = normalize(hidden, gain_two, offset_two)
    rows_two = normed_two.astype(jnp.bfloat16)
    first_layer, second_layer = (
        lax.all_gather(expert_in, "dp", axis=2, tiled=True),
        lax.all_gather(expert_out, "dp", axis=1, tiled=True),
    )
    rows_all, cot_all = (
        lax.all_gather(rows_two, "tensor", axis=0, tiled=True),
        lax.all_gather(cotangent, "tensor", axis=0, tiled=True),
    )
    part_out, part_back, grad_first, grad_second = expert_pass(
        rows_all, cot_all, expert_ids, gate_weights, first_layer, second_layer
    )
    branch_two, back_two = (
        lax.psum_scatter(
            part_out.astype(jnp.bfloat16), "tensor", scatter_dimension=0, tiled=True
        ).astype(jnp.float32),
        lax.psum_scatter(
            part_back.astype(jnp.bfloat16), "tensor", scatter_dimension=0, tiled=True
        ).astype(jnp.float32),
    )
    grad_in, grad_out = (
        lax.psum_scatter(grad_first, "dp", scatter_dimension=2, tiled=True),
        lax.psum_scatter(grad_second, "dp", scatter_dimension=1, tiled=True),
    )
    output = (hidden + branch_two).astype(jnp.bfloat16)
    back_hidden, dgain_two, doffset_two = norm_backward(back_two, scaled_two, inverse_two, gain_two)
    grad_hidden = cotangent.astype(jnp.float32) + back_hidden
    cot_rows = lax.all_gather(grad_hidden.astype(jnp.bfloat16), "tensor", axis=0, tiled=True)
    grad_proj = lax.dot_general(
        blended_rows, cot_rows, (((0,), (0,)), ((), ())), preferred_element_type=jnp.float32
    )
    grad_mixed = lax.dot_general(
        cot_rows, out_matrix, (((1,), (1,)), ((), ())), preferred_element_type=jnp.float32
    ).astype(jnp.bfloat16)
    grad_blocks = grad_mixed.reshape(block_count, IMG_BLOCK, SEQ, local_heads, HEAD_DIM)
    grad_packed = lax.map(attend_backward, (stacked, log_total, grad_blocks)).reshape(
        group_rows, 3 * local_width
    )
    grad_joint = lax.dot_general(
        rows_one, grad_packed, (((0,), (0,)), ((), ())), preferred_element_type=jnp.float32
    )
    back_one = lax.psum_scatter(
        lax.dot_general(
            grad_packed, joint_matrix, (((1,), (1,)), ((), ())), preferred_element_type=jnp.float32
        ).astype(jnp.bfloat16),
        "tensor",
        scatter_dimension=0,
        tiled=True,
    ).astype(jnp.float32)
    grad_norm, dgain_one, doffset_one = norm_backward(back_one, scaled_one, inverse_one, gain_one)
    grad_tokens = grad_hidden + grad_norm
    joint_grad, proj_grad, part_gain_one, part_offset_one, part_gain_two, part_offset_two = (
        lax.psum_scatter(
            grad_joint.reshape(features, 3, local_width), "dp", scatter_dimension=0, tiled=True
        ),
        lax.psum_scatter(grad_proj, "dp", scatter_dimension=1, tiled=True),
        lax.psum_scatter(dgain_one, "dp", scatter_dimension=0, tiled=True),
        lax.psum_scatter(doffset_one, "dp", scatter_dimension=0, tiled=True),
        lax.psum_scatter(dgain_two, "dp", scatter_dimension=0, tiled=True),
        lax.psum_scatter(doffset_two, "dp", scatter_dimension=0, tiled=True),
    )
    sum_gain_one, sum_offset_one, sum_gain_two, sum_offset_two = lax.psum(
        (part_gain_one, part_offset_one, part_gain_two, part_offset_two), "tensor"
    )
    return (
        output,
        grad_tokens,
        joint_grad,
        proj_grad,
        sum_gain_one,
        sum_offset_one,
        sum_gain_two,
        sum_offset_two,
        grad_in,
        grad_out,
    )


def solution(mesh):
    return jax.shard_map(
        on_device,
        mesh=mesh,
        in_specs=(
            P(("dp", "tensor"), None),
            P("dp", None, "tensor"),
            P("tensor", "dp"),
            P("dp"),
            P("dp"),
            P("dp"),
            P("dp"),
            P(None, None, ("dp", "tensor")),
            P(None, ("dp", "tensor"), None),
            P("dp", None),
            P("dp", None),
            P(("dp", "tensor"), None),
        ),
        out_specs=(
            P(("dp", "tensor"), None),
            P(("dp", "tensor"), None),
            P("dp", None, "tensor"),
            P("tensor", "dp"),
            P("dp"),
            P("dp"),
            P("dp"),
            P("dp"),
            P(None, None, ("dp", "tensor")),
            P(None, ("dp", "tensor"), None),
        ),
        check_vma=False,
    )
```

profile of v0, /device:TPU:0, one launch (start us, length us, event | category | flops | bytes accessed | tf_op | source)
XLA Modules:
  0.0 1472.9 jit_solution(13205619504904384404)
XLA Ops:
  12.7 34.9 %all-reduce.21 = (bf16[384]{0:T(512)(128)(2,1)S(1)}, bf16[384]{0:T(512)(128)(2,1)S(1)}, bf16[384]{0:T(512)(128)(2,1)S(1)}, bf16[384]{0:T(512)(128)(2,1)S(1)}) all-reduce(bf16[384]{0:T(512)(128)(2,1)S(1)} %dynamic-update-slice.3, bf16[384]{0:T(512)(128)(2,1)S(1)} %dynamic-update-slice.2, ...), channel_id=1, replica_groups=mesh['dp'=16,'tensor'=2] {'dp'}, use_global_device_ids=true, to_apply=%add.6 | all-reduce | flops 1536 | bytes 6144
  55.1 18.9 %all_gather.39 = bf16[384,3,192]{2,0,1:T(8,128)(2,1)S(1)} all-gather(bf16[24,3,192]{2,0,1:T(8,128)(2,1)S(1)} %copy-done.28), channel_id=1, replica_groups=mesh['dp'=16,'tensor'=2] {'dp'}, dimensions={0}, use_global_device_ids=true | all-gather | bytes 470016 | tf_op jit(solution)/shard_map/all_gather | solution.py:156
  74.3 21.4 %all_gather.40 = bf16[192,384]{0,1:T(8,128)(2,1)} all-gather(bf16[192,24]{0,1:T(8,128)(2,1)S(1)} %copy-done.32), channel_id=1, replica_groups=mesh['dp'=16,'tensor'=2] {'dp'}, dimensions={1}, use_global_device_ids=true | all-gather | bytes 156672 | tf_op jit(solution)/shard_map/all_gather | solution.py:157
  105.9 10.9 reshape.239
  123.2 20.3 %while.38 = (s32[]{:T(128)}, bf16[5,4,197,3,64]{2,1,0,4,3:T(4,128)(2,1)S(1)}, f32[5,4,3,197]{3,2,1,0:T(4,128)}, bf16[5,4,197,3,3,64]{2,5,4,1,3,0:T(8,128)(2,1)}, s32[]{:T(128)}) while((s32[]{:T(128)}, bf16[5,4,197,3,64]{2,1,0,4,3:T(4,128)(2,1)S(1)}, f32[5,4,3,197]{3,2,1,0:T(4,128)}, bf16[5,4,197,3,3,64]{2,5,4,1,3,0:T(8,128)(2,1)}, ...), condition=%wide.region_5.6_spmd, body=%wide.region_2.5_spmd.sunk | while | flops 123095840 | bytes 10357573 | solution.py:175
  151.0 41.3 %fusion = bf16[1984,384]{1,0:T(8,128)(2,1)} fusion(bf16[3940,384]{1,0:T(8,128)(2,1)} %convolution_convert_fusion.4), kind=kCustom, calls=%all-reduce-scatter | all-reduce-scatter fusion | flops 1523713 | bytes 4550144
  219.7 36.9 %scatter_custom_fusion.3 = f32[9856]{0:T(1024)S(1)} fusion(s32[7880]{0:T(1024)S(1)} %fusion.81, f32[7880]{0:T(1024)S(1)} %reshape.293, f32[]{:T(128)} %constant.162.clone.1), kind=kCustom, calls=%fused_computation.158 | custom fusion | bytes 39428 | tf_op jit(solution)/shard_map/scatter | solution.py:99
  256.7 36.9 %scatter_custom_fusion.2 = s32[9856]{0:T(1024)S(1)} fusion(s32[7880]{0:T(1024)S(1)} %fusion.81, s32[7880]{0:T(1024)S(1)} %add_select_fusion, s32[]{:T(128)} %constant.165.clone.1), kind=kCustom, calls=%fused_computation.160 | custom fusion | bytes 39428 | tf_op jit(solution)/shard_map/scatter | solution.py:97
  309.2 7.0 copy.59
  316.3 46.8 %all-gather.13.cloned.1.call-done = bf16[8,768,384]{2,1,0:T(8,128)(2,1)} async-done(((bf16[8,48,384]{2,1,0:T(8,128)(2,1)}), bf16[8,768,384]{2,1,0:T(8,128)(2,1)}) %all-gather.13.cloned.1.call-update) | async-done | bytes 4718608 | tf_op jit(solution)/shard_map/all_gather | solution.py:188
  369.0 572.2 %while.39 = (s32[]{:T(128)}, f32[3941,384]{1,0:T(8,128)}, f32[3941,384]{1,0:T(8,128)}, f32[8,384,768]{1,2,0:T(8,128)}, f32[8,768,384]{2,1,0:T(8,128)}, /*index=5...) while((s32[]{:T(128)}, f32[3941,384]{1,0:T(8,128)}, ...), condition=%wide.region_17.18_spmd, body=%wide.region_14.17_spmd.sunk | while | flops 4435205632 | bytes 57775028 | solution.py:132
  375.9 11.3 fusion.143
  401.7 15.6 %scatter_fusion.1 = f32[3941,384]{1,0:T(8,128)} fusion(f32[3941,384]{1,0:T(8,128)} %get-tuple-element.411, s32[1232]{0:T(1024)S(1)} %fusion.142, f32[1232,384]{1,0:T(8,128)} %fusion.145), kind=kCustom, calls=%fused_computation.3.clone.1 | custom fusion | flops 473088 | bytes 5681984 | tf_op jit(solution)/shard_map/while/body/eval_jaxpr/scatter-add | solution.py:128
  424.9 15.4 %scatter_fusion = f32[3941,384]{1,0:T(8,128)} fusion(f32[3941,384]{1,0:T(8,128)} %get-tuple-element.410, s32[1232]{0:T(1024)S(1)} %fusion.142, f32[1232,384]{1,0:T(8,128)} %convolution_multiply_fusion.5), kind=kCustom, calls=%fused_computation.2.clone.1 | custom fusion | flops 473088 | bytes 5681984 | tf_op jit(solution)/shard_map/while/body/eval_jaxpr/scatter-add | solution.py:127
  447.0 11.3 fusion.143
  472.8 15.9 %scatter_fusion.1 = f32[3941,384]{1,0:T(8,128)} fusion(f32[3941,384]{1,0:T(8,128)} %get-tuple-element.411, s32[1232]{0:T(1024)S(1)} %fusion.142, f32[1232,384]{1,0:T(8,128)} %fusion.145), kind=kCustom, calls=%fused_computation.3.clone.1 | custom fusion | flops 473088 | bytes 5681984 | tf_op jit(solution)/shard_map/while/body/eval_jaxpr/scatter-add | solution.py:128
  496.4 15.7 %scatter_fusion = f32[3941,384]{1,0:T(8,128)} fusion(f32[3941,384]{1,0:T(8,128)} %get-tuple-element.410, s32[1232]{0:T(1024)S(1)} %fusion.142, f32[1232,384]{1,0:T(8,128)} %convolution_multiply_fusion.5), kind=kCustom, calls=%fused_computation.2.clone.1 | custom fusion | flops 473088 | bytes 5681984 | tf_op jit(solution)/shard_map/while/body/eval_jaxpr/scatter-add | solution.py:127
  518.7 11.3 fusion.143
  544.6 15.5 %scatter_fusion.1 = f32[3941,384]{1,0:T(8,128)} fusion(f32[3941,384]{1,0:T(8,128)} %get-tuple-element.411, s32[1232]{0:T(1024)S(1)} %fusion.142, f32[1232,384]{1,0:T(8,128)} %fusion.145), kind=kCustom, calls=%fused_computation.3.clone.1 | custom fusion | flops 473088 | bytes 5681984 | tf_op jit(solution)/shard_map/while/body/eval_jaxpr/scatter-add | solution.py:128
  567.7 15.3 %scatter_fusion = f32[3941,384]{1,0:T(8,128)} fusion(f32[3941,384]{1,0:T(8,128)} %get-tuple-element.410, s32[1232]{0:T(1024)S(1)} %fusion.142, f32[1232,384]{1,0:T(8,128)} %convolution_multiply_fusion.5), kind=kCustom, calls=%fused_computation.2.clone.1 | custom fusion | flops 473088 | bytes 5681984 | tf_op jit(solution)/shard_map/while/body/eval_jaxpr/scatter-add | solution.py:127
  589.7 11.3 fusion.143
  615.5 15.7 %scatter_fusion.1 = f32[3941,384]{1,0:T(8,128)} fusion(f32[3941,384]{1,0:T(8,128)} %get-tuple-element.411, s32[1232]{0:T(1024)S(1)} %fusion.142, f32[1232,384]{1,0:T(8,128)} %fusion.145), kind=kCustom, calls=%fused_computation.3.clone.1 | custom fusion | flops 473088 | bytes 5681984 | tf_op jit(solution)/shard_map/while/body/eval_jaxpr/scatter-add | solution.py:128
  638.9 15.6 %scatter_fusion = f32[3941,384]{1,0:T(8,128)} fusion(f32[3941,384]{1,0:T(8,128)} %get-tuple-element.410, s32[1232]{0:T(1024)S(1)} %fusion.142, f32[1232,384]{1,0:T(8,128)} %convolution_multiply_fusion.5), kind=kCustom, calls=%fused_computation.2.clone.1 | custom fusion | flops 473088 | bytes 5681984 | tf_op jit(solution)/shard_map/while/body/eval_jaxpr/scatter-add | solution.py:127
  661.2 11.3 fusion.143
  687.1 15.5 %scatter_fusion.1 = f32[3941,384]{1,0:T(8,128)} fusion(f32[3941,384]{1,0:T(8,128)} %get-tuple-element.411, s32[1232]{0:T(1024)S(1)} %fusion.142, f32[1232,384]{1,0:T(8,128)} %fusion.145), kind=kCustom, calls=%fused_computation.3.clone.1 | custom fusion | flops 473088 | bytes 5681984 | tf_op jit(solution)/shard_map/while/body/eval_jaxpr/scatter-add | solution.py:128
  710.2 15.3 %scatter_fusion = f32[3941,384]{1,0:T(8,128)} fusion(f32[3941,384]{1,0:T(8,128)} %get-tuple-element.410, s32[1232]{0:T(1024)S(1)} %fusion.142, f32[1232,384]{1,0:T(8,128)} %convolution_multiply_fusion.5), kind=kCustom, calls=%fused_computation.2.clone.1 | custom fusion | flops 473088 | bytes 5681984 | tf_op jit(solution)/shard_map/while/body/eval_jaxpr/scatter-add | solution.py:127
  732.2 11.3 fusion.143
  758.0 16.1 %scatter_fusion.1 = f32[3941,384]{1,0:T(8,128)} fusion(f32[3941,384]{1,0:T(8,128)} %get-tuple-element.411, s32[1232]{0:T(1024)S(1)} %fusion.142, f32[1232,384]{1,0:T(8,128)} %fusion.145), kind=kCustom, calls=%fused_computation.3.clone.1 | custom fusion | flops 473088 | bytes 5681984 | tf_op jit(solution)/shard_map/while/body/eval_jaxpr/scatter-add | solution.py:128
  781.8 15.9 %scatter_fusion = f32[3941,384]{1,0:T(8,128)} fusion(f32[3941,384]{1,0:T(8,128)} %get-tuple-element.410, s32[1232]{0:T(1024)S(1)} %fusion.142, f32[1232,384]{1,0:T(8,128)} %convolution_multiply_fusion.5), kind=kCustom, calls=%fused_computation.2.clone.1 | custom fusion | flops 473088 | bytes 5681984 | tf_op jit(solution)/shard_map/while/body/eval_jaxpr/scatter-add | solution.py:127
  804.3 11.3 fusion.143
  830.2 15.9 %scatter_fusion.1 = f32[3941,384]{1,0:T(8,128)} fusion(f32[3941,384]{1,0:T(8,128)} %get-tuple-element.411, s32[1232]{0:T(1024)S(1)} %fusion.142, f32[1232,384]{1,0:T(8,128)} %fusion.145), kind=kCustom, calls=%fused_computation.3.clone.1 | custom fusion | flops 473088 | bytes 5681984 | tf_op jit(solution)/shard_map/while/body/eval_jaxpr/scatter-add | solution.py:128
  853.7 15.7 %scatter_fusion = f32[3941,384]{1,0:T(8,128)} fusion(f32[3941,384]{1,0:T(8,128)} %get-tuple-element.410, s32[1232]{0:T(1024)S(1)} %fusion.142, f32[1232,384]{1,0:T(8,128)} %convolution_multiply_fusion.5), kind=kCustom, calls=%fused_computation.2.clone.1 | custom fusion | flops 473088 | bytes 5681984 | tf_op jit(solution)/shard_map/while/body/eval_jaxpr/scatter-add | solution.py:127
  876.1 11.3 fusion.143
  902.0 15.7 %scatter_fusion.1 = f32[3941,384]{1,0:T(8,128)} fusion(f32[3941,384]{1,0:T(8,128)} %get-tuple-element.411, s32[1232]{0:T(1024)S(1)} %fusion.142, f32[1232,384]{1,0:T(8,128)} %fusion.145), kind=kCustom, calls=%fused_computation.3.clone.1 | custom fusion | flops 473088 | bytes 5681984 | tf_op jit(solution)/shard_map/while/body/eval_jaxpr/scatter-add | solution.py:128
  925.4 15.5 %scatter_fusion = f32[3941,384]{1,0:T(8,128)} fusion(f32[3941,384]{1,0:T(8,128)} %get-tuple-element.410, s32[1232]{0:T(1024)S(1)} %fusion.142, f32[1232,384]{1,0:T(8,128)} %convolution_multiply_fusion.5), kind=kCustom, calls=%fused_computation.2.clone.1 | custom fusion | flops 473088 | bytes 5681984 | tf_op jit(solution)/shard_map/while/body/eval_jaxpr/scatter-add | solution.py:127
  946.0 41.4 %fusion.2 = bf16[1984,384]{1,0:T(8,128)(2,1)} fusion(bf16[3940,384]{1,0:T(8,128)(2,1)} %slice.80), kind=kCustom, calls=%all-reduce-scatter.2 | all-reduce-scatter fusion | flops 1523713 | bytes 4550144
  991.9 8.4 concatenate.18
  1011.6 39.0 %all-gather.21.cloned.1.call-done = bf16[2,1970,384]{2,1,0:T(8,128)(2,1)} async-done(((bf16[1,1970,384]{2,1,0:T(8,128)(2,1)}), bf16[2,1970,384]{2,1,0:T(8,128)(2,1)}) %all-gather.21.cloned.1.call-update) | async-done | bytes 3025936 | tf_op jit(solution)/shard_map/all_gather | solution.py:212
  1065.7 42.7 %while.40 = (s32[]{:T(128)}, bf16[5,4,197,3,3,64]{2,1,0,5,4,3:T(4,128)(2,1)}, bf16[5,4,197,3,3,64]{2,5,4,1,3,0:T(8,128)(2,1)}, f32[5,4,3,197]{3,2,1,0:T(4,128)}, bf16[5,4,197,3,64]{2,1,0,4,3:T(4,128)(2,1)}, /*index=5*/s32[]{:T(128)}) while((s32[]{:T(128)}, bf16[5,4,197,3,3,64]{2,1,0,5,4,3:T(4,128)(2,1)}, ...), condition=%wide.region_24.25_spmd, body=%wide.region_22.24_spmd.sunk | while | flops 303440672 | bytes 25108952 | solution.py:220
  1108.5 9.6 reshape.247
  1131.4 7.3 convolution_convert_fusion.3
  1138.7 73.4 %fusion.86 = (bf16[1984,384]{1,0:T(8,128)(2,1)}, bf16[1984,384]{1,0:T(8,128)(2,1)}) fusion(bf16[3940,384]{1,0:T(8,128)(2,1)} %slice.81, bf16[3940,384]{1,0:T(8,128)(2,1)} %convolution_convert_fusion.3), kind=kCustom, calls=%all-reduce-scatter.4 | all-reduce-scatter fusion | flops 3047425 | bytes 9099776
  1217.9 8.3 concatenate.19
  1229.5 32.5 %all-reduce.19 = (f32[384]{0:T(512)S(1)}, f32[384]{0:T(512)S(1)}, f32[384]{0:T(512)S(1)}, f32[384]{0:T(512)S(1)}) all-reduce(f32[384]{0:T(512)S(1)} %get-tuple-element.167, f32[384]{0:T(512)S(1)} %get-tuple-element.172, f32[384]{0:T(512)S(1)} %get-tuple-element.165, ...), channel_id=8, replica_groups=mesh['dp'=16,'tensor'=2] {'dp'}, use_global_device_ids=true, to_apply=%region_31.32.clone | all-reduce | flops 1536 | bytes 12288
  1262.3 8.3 concatenate.17
  1276.0 8.0 fusion.64
  1284.1 66.4 %reduce-scatter.17.cloned.1.call-done = f32[8,384,48]{1,2,0:T(8,128)} async-done(((f32[8,384,768]{1,2,0:T(8,128)}), f32[8,384,48]{1,2,0:T(8,128)}) %reduce-scatter.17.cloned.1.call-update) | async-done | bytes 589840 | tf_op jit(solution)/shard_map/reduce_scatter | solution.py:206
  1350.5 115.4 %reduce-scatter.19.cloned.1.call-done = f32[8,48,384]{2,1,0:T(8,128)} async-done(((f32[8,768,384]{2,1,0:T(8,128)}), f32[8,48,384]{2,1,0:T(8,128)}) %reduce-scatter.19.cloned.1.call-update) | async-done | bytes 589840 | tf_op jit(solution)/shard_map/reduce_scatter | solution.py:207
  (383 shorter events, 441.4 us)
Async XLA Ops:
  7.2 45.0 %copy-start = (bf16[1970,384]{1,0:T(8,128)(2,1)S(1)}, bf16[1970,384]{1,0:T(8,128)(2,1)}, u32[]{:S(2)}) copy-start(bf16[1970,384]{1,0:T(8,128)(2,1)} %param.18) | copy-start | bytes 4538884
  7.2 88.5 %all-gather.15.cloned.1.call-start = ((), (), s32[]{:S(2)}) async-start(), calls=%async_computation.10 | async-start | bytes 4552704 | tf_op jit(solution)/shard_map/all_gather | solution.py:168
  47.6 6.6 copy-start.29
  54.2 20.1 %copy-start.32 = (bf16[192,24]{0,1:T(8,128)(2,1)S(1)}, bf16[192,24]{0,1:T(8,128)(2,1)}, u32[]{:S(2)}) copy-start(bf16[192,24]{0,1:T(8,128)(2,1)} %param.20) | copy-start | bytes 27652
  54.3 239.4 %all-gather.19.cloned.1.call-start = ((), (), s32[]{:S(2)}) async-start(), calls=%async_computation.12 | async-start | bytes 4552704 | tf_op jit(solution)/shard_map/all_gather | solution.py:192
  55.0 245.0 %all-gather.17.cloned.1.call-start = ((), (), s32[]{:S(2)}) async-start(), calls=%async_computation.11 | async-start | bytes 4552704 | tf_op jit(solution)/shard_map/all_gather | solution.py:191
  74.3 25.5 %copy-start.14 = (bf16[384,3,192]{0,2,1:T(8,128)(2,1)}, bf16[384,3,192]{0,2,1:T(8,128)(2,1)S(1)}, u32[]{:S(2)}) copy-start(bf16[384,3,192]{0,2,1:T(8,128)(2,1)S(1)} %copy.51) | copy-start | bytes 1327108
  116.8 6.4 copy-start.10
  151.0 44.9 %copy-start.33 = (u32[32]{0:T(128)S(1)}, u32[32]{0:T(128)}, u32[]{:S(2)}) copy-start(u32[32]{0:T(128)} %constant.215) | copy-start | bytes 388
  193.0 4.2 collective-permute-start
  197.2 9.1 copy-start.26
  209.1 100.2 %all-gather.11.cloned.1.call-start = ((), (), s32[]{:S(2)}) async-start(), calls=%async_computation.4 | async-start | bytes 5013504 | tf_op jit(solution)/shard_map/all_gather | solution.py:187
  209.9 153.2 %all-gather.13.cloned.1.call-start = ((), (), s32[]{:S(2)}) async-start(), calls=%async_computation.5 | async-start | bytes 5013504 | tf_op jit(solution)/shard_map/all_gather | solution.py:188
  210.5 840.0 %all-gather.21.cloned.1.call-start = ((), (), s32[]{:S(2)}) async-start(), calls=%async_computation.13 | async-start | bytes 4552704 | tf_op jit(solution)/shard_map/all_gather | solution.py:212
  212.4 5.3 copy-start.31
  417.2 4.2 copy-start.34
  462.9 4.1 copy-start.6
  488.7 4.2 copy-start.34
  534.6 4.1 copy-start.6
  560.1 4.2 copy-start.34
  605.6 4.1 copy-start.6
  631.3 4.2 copy-start.34
  677.1 4.1 copy-start.6
  702.5 4.2 copy-start.34
  748.1 4.1 copy-start.6
  774.1 4.2 copy-start.34
  846.0 4.2 copy-start.34
  892.0 4.1 copy-start.6
  917.7 4.2 copy-start.34
  945.9 54.3 %copy-start.1 = (bf16[1970,384]{1,0:T(8,128)(2,1)S(1)}, bf16[1970,384]{1,0:T(8,128)(2,1)}, u32[]{:S(2)}) copy-start(bf16[1970,384]{1,0:T(8,128)(2,1)} %param.18) | copy-start | bytes 4538884
  945.9 54.3 %copy-start.3 = (bf16[1998,384]{1,0:T(8,128)(2,1)S(1)}, bf16[1998,384]{1,0:T(8,128)(2,1)}, u32[]{:S(2)}) copy-start(bf16[1998,384]{1,0:T(8,128)(2,1)} %copy-done.2) | copy-start | bytes 4603396
  945.9 54.3 %copy-start.18 = (f32[1970]{0:T(1024)S(1)}, f32[1970]{0:T(1024)}, u32[]{:S(2)}) copy-start(f32[1970]{0:T(1024)} %copy-done.17) | copy-start | bytes 23644
  945.9 54.3 %copy-start.22 = (f32[1970]{0:T(1024)S(1)}, f32[1970]{0:T(1024)}, u32[]{:S(2)}) copy-start(f32[1970]{0:T(1024)} %copy-done.21) | copy-start | bytes 23644
  945.9 54.3 %copy-start.27 = (f32[384]{0:T(512)S(1)}, f32[384]{0:T(512)}, u32[]{:S(2)}) copy-start(f32[384]{0:T(512)} %copy-done.26) | copy-start | bytes 4612
  988.0 3.8 collective-permute-start.2
  1007.4 276.6 %reduce-scatter.15.cloned.1.call-start = ((), (), s32[]{:S(2)}) async-start(), calls=%async_computation.7 | async-start | bytes 417792 | tf_op jit(solution)/shard_map/reduce_scatter | solution.py:240
  1011.5 43.0 %copy-start.13 = (bf16[192,384]{0,1:T(8,128)(2,1)S(1)}, bf16[192,384]{0,1:T(8,128)(2,1)}, u32[]{:S(2)}) copy-start(bf16[192,384]{0,1:T(8,128)(2,1)} %all_gather.40) | copy-start | bytes 442372
  1054.6 4.4 copy-start.4
  1054.6 4.4 copy-start.9
  1118.1 165.9 %reduce-scatter.13.cloned.1.call-start = ((), (), s32[]{:S(2)}) async-start(), calls=%async_computation.6 | async-start | bytes 1253376 | tf_op jit(solution)/shard_map/reduce_scatter | solution.py:237
  1125.3 225.2 %reduce-scatter.17.cloned.1.call-start = ((), (), s32[]{:S(2)}) async-start(), calls=%async_computation.8 | async-start | bytes 10027008 | tf_op jit(solution)/shard_map/reduce_scatter | solution.py:206
  1126.0 339.8 %reduce-scatter.19.cloned.1.call-start = ((), (), s32[]{:S(2)}) async-start(), calls=%async_computation.9 | async-start | bytes 10027008 | tf_op jit(solution)/shard_map/reduce_scatter | solution.py:207
  1126.6 4.8 copy-start.15
  1212.1 14.2 copy-start.20
  1212.1 14.2 copy-start.24
  1212.1 14.2 copy-start.30
  1212.8 5.1 collective-permute-start.3
  1216.6 45.7 %collective-permute-start.1 = (bf16[14,384]{1,0:T(8,128)(2,1)S(1)}, bf16[14,384]{1,0:T(8,128)(2,1)S(1)}, u32[]{:S(2)}, u32[]{:S(2)}) collective-permute-start(bf16[14,384]{1,0:T(8,128)(2,1)S(1)} %slice.55), channel_id=1, source_target_pairs={{0,1},{2,3},{4,5},{6,7},{8,9},{10,11},{12,13},{14,15},{16,17},{18,... | collective-permute-start | bytes 32264
  (15 other events, 39.1 us)
Sparse Core Ops, SparseCore 0:
  54.4 40.9 all-gather.14
  96.9 43.6 all-gather.18
  209.2 44.1 all-gather.16
  256.1 53.1 all-gather.10
  311.3 51.7 all-gather.12
  1007.5 42.9 all-gather.20
  1118.3 55.9 reduce-scatter.14
  1178.5 57.1 reduce-scatter.12
  1240.3 110.1 reduce-scatter.16
  1355.0 110.7 reduce-scatter.18
where the time goes:
time: 1490 us; the launch traced here: 1470 us
  local copies, waits for them, and re-layouts  333 us (22%)
  other arithmetic  291 us (20%)
  matrix products  279 us (19%)
  waiting for transfers between devices  273 us (18%)
  blocking collectives  269 us (18%)
  between operations  17 us (1%)
    unnamed x5, blocking collectives  223 us
    scatter-add x8, other arithmetic, per_expert(): back_sum = back_sum.at[slot_rows].add(grad_loaded)  126 us
    scatter-add x8, other arithmetic, per_expert(): out_sum = out_sum.at[slot_rows].add(results * slot_gate[:, None])  125 us
    reduce_scatter x1, waiting for transfers between devices, on_device(): lax.psum_scatter(grad_second, 'dp', scatter_dimension=1, tiled=True)  115 us
    dot_general x8, matrix products, per_expert(): jnp.dot(loaded, first_piece, preferred_element_type=jnp.float32)  90 us
    reduce_scatter x1, waiting for transfers between devices, on_device(): lax.psum_scatter(grad_first, 'dp', scatter_dimension=2, tiled=True)  66.4 us
    unnamed x97, local copies, waits for them, and re-layouts  65.6 us
    gather x8, local copies, waits for them, and re-layouts, per_expert(): loaded = padded[slot_rows]  53 us
  transfers between devices with their start and end apart: 14, of which 6 were waited for; matrix products, arithmetic and copies ran while one was open for 23% of the time, Pallas kernels for 0%

commit v1 on v0

v1 whole, which is shorter than its diff:
```python
import functools

import jax
import jax.numpy as jnp
from jax import lax
from jax.experimental import pallas as pl
from jax.experimental.pallas import tpu as pltpu
from jax.sharding import Mesh
from jax.sharding import PartitionSpec as P

HEAD_DIM = 64
SEQ = 197
EPSILON = 1e-06
ALIGN = 16
WIN = 224
CHUNK = 256
BLOCKS = 4
NEG = -1e30
F32 = jnp.float32
BF16 = jnp.bfloat16
INV_ROOT_TAU = 0.3989422804014327
ALL = ("chip", "core", "tensor")
DP = ("chip", "core")
RING = ("chip", "tensor")
SWAP = [(0, 1), (1, 0)]
VMEM_LIMIT = 60 * 1024 * 1024


def nn(a, b):
    return lax.dot_general(a, b, (((1,), (0,)), ((), ())), preferred_element_type=F32)


def nt(a, b):
    return lax.dot_general(a, b, (((1,), (1,)), ((), ())), preferred_element_type=F32)


def tn(a, b):
    return lax.dot_general(a, b, (((0,), (0,)), ((), ())), preferred_element_type=F32)


def standardize(matrix):
    centre = matrix - jnp.mean(matrix, -1, keepdims=True)
    variance = jnp.mean(centre * centre, -1, keepdims=True)
    inverse = lax.rsqrt(variance + EPSILON)
    return centre * inverse, inverse


def norm_back(weighted, scaled, inverse):
    return inverse * (
        weighted
        - jnp.mean(weighted, -1, keepdims=True)
        - scaled * jnp.mean(weighted * scaled, -1, keepdims=True)
    )


def window(i):
    first = i * SEQ
    start = pl.multiple_of((first // ALIGN) * ALIGN, ALIGN)
    return start, first - start


def put(ref, start, keep, value):
    head = pl.ds(start, ALIGN)
    ref[head, :] = jnp.where(keep, value[:ALIGN], ref[head, :])
    ref[pl.ds(start + ALIGN, WIN - ALIGN), :] = value[ALIGN:]


def fill(dst, src, rows):
    padded = dst.shape[0]
    dst[padded - ALIGN :, :] = jnp.zeros((ALIGN, dst.shape[1]), dst.dtype)
    dst[0:rows, :] = src[...]


def masks(offset):
    row = lax.broadcasted_iota(jnp.int32, (WIN, 1), 0)
    col = lax.broadcasted_iota(jnp.int32, (1, WIN), 1)
    valid = (row >= offset) & (row < offset + SEQ)
    bias = jnp.where((col >= offset) & (col < offset + SEQ), 0.0, NEG).astype(F32)
    keep = lax.broadcasted_iota(jnp.int32, (ALIGN, 1), 0) >= offset
    return valid, bias, keep


def attention_forward(tok, wqkv, wout, par, normed_o, hidden_o, packed_o, mixed_o, lse_o, xs):
    rows, width = tok.shape
    fill(xs, tok, rows)
    lane = lax.broadcasted_iota(jnp.int32, (1, 128), 1)
    low = lane < HEAD_DIM
    gain1, shift1, gain2, shift2 = (par[k : k + 1, :] for k in range(4))

    def image(i, carry):
        start, offset = window(i)
        valid, bias, keep = masks(offset)
        x = xs[pl.ds(start, WIN), :].astype(F32)
        scaled1, _ = standardize(x)
        normed1 = (scaled1 * gain1 + shift1).astype(BF16)
        packed = nn(normed1, wqkv[...]).astype(BF16)
        pieces = []
        lse = jnp.zeros((WIN, 128), F32)
        for pair in range(width // 128):
            at = 128 * pair
            q2 = packed[:, at : at + 128]
            k2 = packed[:, width + at : width + at + 128]
            v2 = packed[:, 2 * width + at : 2 * width + at + 128]
            halves = []
            for half in range(2):
                mine = low if half == 0 else ~low
                qm = jnp.where(mine, q2, jnp.zeros_like(q2)) * jnp.asarray(0.125, BF16)
                s = nt(qm, k2) + bias
                top = jnp.max(s, -1, keepdims=True)
                e = jnp.exp(s - top)
                total = jnp.sum(e, -1, keepdims=True)
                halves.append(nn(e.astype(BF16), v2) * (1.0 / total))
                lse = jnp.where(lane == 2 * pair + half, top + jnp.log(total), lse)
            pieces.append(jnp.where(low, halves[0], halves[1]).astype(BF16))
        mixed = jnp.concatenate(pieces, -1)
        hidden = x + nn(mixed, wout[...])
        scaled2, _ = standardize(hidden)
        put(normed_o, start, keep, (scaled2 * gain2 + shift2).astype(BF16))
        put(hidden_o, start, keep, hidden)
        put(packed_o, start, keep, packed)
        put(mixed_o, start, keep, mixed)
        put(lse_o, start, keep, lse)
        return carry

    lax.fori_loop(0, rows // SEQ, image, 0)


def attention_backward(
    tok, cot, hidden_r, packed_r, mixed_r, lse_r, own, other, wqkv, wout, par,
    out_o, gtok_o, gqkv_o, gout_o, gpar_o, xs, cs, outs, gtoks,
):
    rows, width = tok.shape
    fill(xs, tok, rows)
    fill(cs, cot, rows)
    gqkv_o[...] = jnp.zeros_like(gqkv_o)
    gout_o[...] = jnp.zeros_like(gout_o)
    gpar_o[...] = jnp.zeros_like(gpar_o)
    lane = lax.broadcasted_iota(jnp.int32, (1, 128), 1)
    low = lane < HEAD_DIM
    gain1, shift1, gain2 = (par[k : k + 1, :] for k in range(3))
    eighth = jnp.asarray(0.125, BF16)

    def image(i, carry):
        start, offset = window(i)
        valid, bias, keep = masks(offset)
        here = pl.ds(start, WIN)
        hidden = hidden_r[here, :]
        put(
            outs, start, keep,
            (hidden + own[here, 0:width].astype(F32) + other[here, 0:width].astype(F32)).astype(BF16),
        )
        scaled2, inverse2 = standardize(hidden)
        g2 = own[here, width:].astype(F32) + other[here, width:].astype(F32)
        g2 = jnp.where(valid, g2, 0.0)
        gpar_o[2:3, :] += jnp.sum(g2 * scaled2, 0, keepdims=True)
        gpar_o[3:4, :] += jnp.sum(g2, 0, keepdims=True)
        ghid = cs[here, :].astype(F32) + norm_back(g2 * gain2, scaled2, inverse2)
        branch = jnp.where(valid, ghid, 0.0).astype(BF16)
        gout_o[...] += tn(mixed_r[here, :], branch)
        gmix = nt(branch, wout[...]).astype(BF16)
        gq, gk, gv = [], [], []
        for pair in range(width // 128):
            at = 128 * pair
            q2 = packed_r[here, at : at + 128]
            k2 = packed_r[here, width + at : width + at + 128]
            v2 = packed_r[here, 2 * width + at : 2 * width + at + 128]
            gm2 = gmix[:, at : at + 128]
            sums = [0.0, 0.0, 0.0]
            for half in range(2):
                mine = low if half == 0 else ~low
                qm = jnp.where(mine, q2, jnp.zeros_like(q2)) * eighth
                km = jnp.where(mine, k2, jnp.zeros_like(k2)) * eighth
                gm = jnp.where(mine, gm2, jnp.zeros_like(gm2))
                head = 2 * pair + half
                lse = jnp.where(valid, lse_r[here, head : head + 1], -NEG)
                p = jnp.exp(nt(qm, k2) + bias - lse)
                gp = nt(gm, v2)
                inner = jnp.sum(gp * p, -1, keepdims=True)
                gs = (p * (gp - inner)).astype(BF16)
                sums[0] += nn(gs, km)
                sums[1] += tn(gs, qm)
                sums[2] += tn(p.astype(BF16), gm)
            for store, total in zip((gq, gk, gv), sums):
                store.append(total.astype(BF16))
        gpacked = jnp.concatenate(gq + gk + gv, -1)
        scaled1, inverse1 = standardize(xs[here, :].astype(F32))
        normed1 = (scaled1 * gain1 + shift1).astype(BF16)
        gqkv_o[...] += tn(normed1, gpacked)
        g1 = nt(gpacked, wqkv[...])
        gpar_o[0:1, :] += jnp.sum(g1 * scaled1, 0, keepdims=True)
        gpar_o[1:2, :] += jnp.sum(g1, 0, keepdims=True)
        put(gtoks, start, keep, ghid + norm_back(g1 * gain1, scaled1, inverse1))
        return carry

    lax.fori_loop(0, rows // SEQ, image, 0)
    out_o[...] = outs[0:rows, :]
    gtok_o[...] = gtoks[0:rows, :]


def gelu_parts(v):
    e = jnp.exp(v * v * -0.5)
    t = 1.0 / (1.0 + jnp.abs(v) * (0.3275911 * 0.7071067811865476))
    q = 0.5 * 1.061405429
    for c in (-1.453152027, 1.421413741, -0.284496736, 0.254829592):
        q = q * t + 0.5 * c
    q = q * t * e
    return jnp.where(v < 0, q, 1.0 - q), e * INV_ROOT_TAU


def experts(
    cnt, rown, rsib, cown, csib, town, tsib, w_ref,
    pown, psib, g_ref, xb, gb, tmpx, tmpg, acc1, acc2, off, dst, base, tot,
):
    number = pl.num_programs(0)
    e_now = pl.program_id(0)
    depth = town.shape[2]
    width = rown.shape[1]
    slots = tmpx.shape[0]
    step = slots // 3

    def blocks(fn):
        for side, (table, r, c, out) in enumerate(((town, rown, cown, pown), (tsib, rsib, csib, psib))):
            def body(j, carry, side=side, table=table, r=r, c=c, out=out):
                fn(side * BLOCKS + j, table[j], r, c, out, pl.ds(pl.multiple_of(j * depth, ALIGN), depth))
                return carry

            lax.fori_loop(0, BLOCKS, body, 0)

    def onehot(table, at):
        slot = (lax.broadcasted_iota(jnp.int32, (step, 1), 0) + at).astype(F32)
        first = table[0:1, :] == slot
        second = table[1:2, :] == slot
        gate = jnp.where(first, table[2:3, :], jnp.where(second, table[3:4, :], 0.0))
        pick = jnp.where(first | second, 1.0, 0.0).astype(BF16)
        return pick, jnp.sum(gate, -1, keepdims=True)

    def segments(b, move):
        def per(e, carry):
            k = b * number + e
            o, d = off[k], dst[k]

            def tile(t, carry):
                move(
                    pl.ds(pl.multiple_of(o + t * ALIGN, ALIGN), ALIGN),
                    pl.ds(pl.multiple_of(d + t * ALIGN, ALIGN), ALIGN),
                )
                return carry

            return lax.fori_loop(0, (cnt[k] + (ALIGN - 1)) // ALIGN, tile, carry)

        lax.fori_loop(0, number, per, 0)

    @pl.when(e_now == 0)
    def _():
        def plan_expert(e, at):
            base[e] = at

            def plan_block(b, run):
                dst[b * number + e] = at + run
                return run + (cnt[b * number + e] + (ALIGN - 1)) // ALIGN * ALIGN

            total = lax.fori_loop(0, 2 * BLOCKS, plan_block, 0)
            tot[e] = total
            return at + (total + (CHUNK - 1)) // CHUNK * CHUNK

        lax.fori_loop(0, number, plan_expert, 0)

        def plan_off(b, carry):
            def one(e, run):
                off[b * number + e] = run
                return run + (cnt[b * number + e] + (ALIGN - 1)) // ALIGN * ALIGN

            lax.fori_loop(0, number, one, 0)
            return carry

        lax.fori_loop(0, 2 * BLOCKS, plan_off, 0)

        def dispatch(b, table, r, c, out, here):
            rows, cots = r[here, :], c[here, :]
            for k in range(3):
                pick, gate = onehot(table, k * step)
                tmpx[k * step : (k + 1) * step, :] = nn(pick, rows).astype(BF16)
                tmpg[k * step : (k + 1) * step, :] = (nn(pick, cots) * gate).astype(BF16)

            def move(local, far):
                xb[far, :] = tmpx[local, :]
                gb[far, :] = tmpg[local, :]

            segments(b, move)

        blocks(dispatch)

        def clear(e, carry):
            total = tot[e]
            end = base[e] + total

            def tile(t, carry):
                far = pl.ds(pl.multiple_of(end + t * ALIGN, ALIGN), ALIGN)
                xb[far, :] = jnp.zeros((ALIGN, width), BF16)
                gb[far, :] = jnp.zeros((ALIGN, width), BF16)
                return carry

            rest = (total + (CHUNK - 1)) // CHUNK * CHUNK - total
            return lax.fori_loop(0, rest // ALIGN, tile, carry)

        lax.fori_loop(0, number, clear, 0)

    shards, _, _, units, _ = w_ref.shape
    hidden = shards * units
    acc1[...] = jnp.zeros_like(acc1)
    acc2[...] = jnp.zeros_like(acc2)

    def chunk(t, carry):
        here = pl.ds(pl.multiple_of(base[e_now] + t * CHUNK, ALIGN), CHUNK)
        first = w_ref[:, 0, 0].reshape(hidden, width)
        second = w_ref[:, 0, 1].reshape(hidden, width)
        x, g = xb[here, :], gb[here, :]
        v = nt(x, first)
        big, small = gelu_parts(v)
        act = (v * big).astype(BF16)
        gpre = (nt(g, second) * (big + v * small)).astype(BF16)
        acc1[...] += tn(gpre, x)
        acc2[...] += tn(act, g)
        xb[here, :] = nn(act, second).astype(BF16)
        gb[here, :] = nn(gpre, first).astype(BF16)
        return carry

    lax.fori_loop(0, (tot[e_now] + (CHUNK - 1)) // CHUNK, chunk, 0)
    g_ref[:, 0, 0] = acc1[...].reshape(shards, units, width).astype(BF16)
    g_ref[:, 0, 1] = acc2[...].reshape(shards, units, width).astype(BF16)

    @pl.when(e_now == number - 1)
    def _():
        def combine(b, table, r, c, out, here):
            def move(local, far):
                tmpx[local, :] = xb[far, :]
                tmpg[local, :] = gb[far, :]

            segments(b, move)
            forward, back = 0.0, 0.0
            for k in range(3):
                pick, gate = onehot(table, k * step)
                part = slice(k * step, (k + 1) * step)
                forward += tn(pick, (tmpx[part, :].astype(F32) * gate).astype(BF16))
                back += tn(pick, tmpg[part, :])
            out[here, 0:width] = forward.astype(BF16)
            out[here, width:] = back.astype(BF16)

        blocks(combine)


def route(ids, gates, number, padded):
    rows = ids.shape[1]
    depth = padded // BLOCKS
    ids = jnp.pad(ids, ((0, 0), (0, padded - rows)), constant_values=-1)
    gates = jnp.pad(gates, ((0, 0), (0, padded - rows)))
    ids = ids.reshape(2, BLOCKS, 1, depth)
    gates = gates.reshape(2, BLOCKS, 1, depth)
    match = ids == jnp.arange(number, dtype=jnp.int32)[None, None, :, None]
    named = (match[0] | match[1]).astype(BF16)
    order = jnp.arange(depth)
    earlier = (order[:, None] < order[None, :]).astype(BF16)
    rank = jnp.einsum("ber,rs->bes", named, earlier, preferred_element_type=F32)
    count = jnp.sum(named.astype(F32), -1)
    room = jnp.ceil(count * (1.0 / ALIGN)) * ALIGN
    before = jnp.arange(number)
    off = jnp.sum(jnp.where(before[None, :, None] < before[None, None, :], room[:, :, None], 0.0), 1)
    place = off[:, :, None] + rank
    slot = jnp.sum(jnp.where(match, place[None], 0.0), 2)
    slot = jnp.where(ids[:, :, 0] >= 0, slot, -1.0)
    table = jnp.stack([slot[0], slot[1], gates[0, :, 0], gates[1, :, 0]], 1)
    lanes = jnp.pad(count, ((0, 0), (0, depth - number)))
    return jnp.concatenate([table, lanes[:, None, :], jnp.zeros((BLOCKS, 3, depth), F32)], 1)


def whole(shape, dtype):
    return jax.ShapeDtypeStruct(shape, dtype)


IN_VMEM = pl.BlockSpec(memory_space=pltpu.VMEM)


def on_device(
    tokens, query_key_value, attention_out, first_gain, first_shift, second_gain, second_shift,
    expert_in, expert_out, expert_ids, gate_weights, cotangent,
):
    rows, width = tokens.shape
    padded = -(-rows // (ALIGN * BLOCKS)) * (ALIGN * BLOCKS)
    number = expert_in.shape[0]
    groups, span = lax.axis_size(DP), lax.axis_size("tensor")
    part = width // groups
    wide = width // span
    half = lax.axis_index("tensor")

    small = jnp.concatenate(
        [query_key_value.reshape(-1), attention_out.reshape(-1), first_gain, first_shift, second_gain, second_shift]
    )
    length = small.shape[0]
    rounded = -(-length // 1024) * 1024
    gathered = lax.all_gather(jnp.pad(small, (0, rounded - length)), ALL, axis=0, tiled=False)
    sizes = (query_key_value.size, attention_out.size)
    wqkv = (
        gathered[:, : sizes[0]]
        .reshape(groups, span, part, 3, wide)
        .transpose(0, 2, 3, 1, 4)
        .reshape(width, 3 * width)
    )
    wout = (
        gathered[:, sizes[0] : sizes[0] + sizes[1]]
        .reshape(groups, span, wide, part)
        .transpose(1, 2, 0, 3)
        .reshape(width, width)
    )
    par = (
        gathered.reshape(groups, span, rounded)[:, 0, sizes[0] + sizes[1] : length]
        .reshape(groups, 4, part)
        .transpose(1, 0, 2)
        .reshape(4, width)
        .astype(F32)
    )
    shard = jnp.stack([expert_in.transpose(0, 2, 1), expert_out], 1)
    weights = lax.all_gather(shard, RING, axis=0, tiled=False)
    shards, units = weights.shape[0], weights.shape[3]
    regroup = units % ALIGN != 0
    if regroup:
        weights = weights.transpose(1, 2, 0, 3, 4).reshape(1, number, 2, shards * units, width)

    ids = lax.dynamic_slice_in_dim(expert_ids.T, half * rows, rows, 1)
    gates = lax.dynamic_slice_in_dim(gate_weights.T, half * rows, rows, 1)
    table = route(ids, gates, number, padded)
    table_sib = lax.ppermute(table, "core", SWAP)
    cot_own = jnp.pad(cotangent, ((0, padded - rows), (0, 0)))
    cot_sib = lax.ppermute(cot_own, "core", SWAP)

    normed, hidden, packed, mixed, lse = pl.pallas_call(
        attention_forward,
        out_shape=(
            whole((padded, width), BF16),
            whole((padded, width), F32),
            whole((padded, 3 * width), BF16),
            whole((padded, width), BF16),
            whole((padded, 128), F32),
        ),
        in_specs=[IN_VMEM] * 4,
        out_specs=(IN_VMEM,) * 5,
        scratch_shapes=[pltpu.VMEM((padded, width), BF16)],
        compiler_params=pltpu.CompilerParams(vmem_limit_bytes=VMEM_LIMIT),
        cost_estimate=pl.CostEstimate(flops=6 * 10**9, bytes_accessed=14 * 10**6, transcendentals=3 * 10**6),
        name="attention_forward",
    )(tokens, wqkv, wout, par)
    normed_sib = lax.ppermute(normed, "core", SWAP)

    counts = jnp.concatenate([table[:, 4, :number], table_sib[:, 4, :number]], 0).astype(jnp.int32).reshape(-1)
    n_blocks = 2 * BLOCKS
    room = -(-(4 * rows + n_blocks * number * (ALIGN - 1) + number * (CHUNK - ALIGN)) // CHUNK) * CHUNK
    depth = padded // BLOCKS
    slots = -(-(2 * depth + number * (ALIGN - 1)) // (3 * ALIGN)) * (3 * ALIGN)
    held = weights.shape[0] * weights.shape[3]

    def full(*shape):
        return pl.BlockSpec(shape, lambda e, *_: (0,) * len(shape), pipeline_mode=pl.Buffered(1))

    by_expert = pl.BlockSpec(
        (weights.shape[0], 1, 2, weights.shape[3], width), lambda e, *_: (0, e, 0, 0, 0)
    )
    part_own, part_sib, grads = pl.pallas_call(
        experts,
        out_shape=(
            whole((padded, 2 * width), BF16),
            whole((padded, 2 * width), BF16),
            whole(weights.shape, BF16),
        ),
        grid_spec=pltpu.PrefetchScalarGridSpec(
            num_scalar_prefetch=1,
            grid=(number,),
            in_specs=[full(padded, width)] * 4 + [full(*table.shape)] * 2 + [by_expert],
            out_specs=(full(padded, 2 * width), full(padded, 2 * width), by_expert),
            scratch_shapes=[
                pltpu.VMEM((room, width), BF16),
                pltpu.VMEM((room, width), BF16),
                pltpu.VMEM((slots, width), BF16),
                pltpu.VMEM((slots, width), BF16),
                pltpu.VMEM((held, width), F32),
                pltpu.VMEM((held, width), F32),
                pltpu.SMEM((n_blocks * number,), jnp.int32),
                pltpu.SMEM((n_blocks * number,), jnp.int32),
                pltpu.SMEM((number,), jnp.int32),
                pltpu.SMEM((number,), jnp.int32),
            ],
        ),
        compiler_params=pltpu.CompilerParams(
            vmem_limit_bytes=VMEM_LIMIT, dimension_semantics=("arbitrary",)
        ),
        cost_estimate=pl.CostEstimate(flops=50 * 10**9, bytes_accessed=40 * 10**6, transcendentals=12 * 10**6),
        name="experts",
    )(counts, normed, normed_sib, cot_own, cot_sib, table, table_sib, weights)
    part_other = lax.ppermute(part_sib, "core", SWAP)
    if regroup:
        grads = grads.reshape(number, 2, shards, units, width).transpose(2, 0, 1, 3, 4)
    grad_shard = lax.psum_scatter(grads, RING, scatter_dimension=0, tiled=False).astype(F32)

    output, grad_tokens, gqkv, gout, gpar = pl.pallas_call(
        attention_backward,
        out_shape=(
            whole((rows, width), BF16),
            whole((rows, width), F32),
            whole((width, 3 * width), F32),
            whole((width, width), F32),
            whole((8, width), F32),
        ),
        in_specs=[IN_VMEM] * 11,
        out_specs=(IN_VMEM,) * 5,
        scratch_shapes=[
            pltpu.VMEM((padded, width), BF16),
            pltpu.VMEM((padded, width), BF16),
            pltpu.VMEM((padded, width), BF16),
            pltpu.VMEM((padded, width), F32),
        ],
        compiler_params=pltpu.CompilerParams(vmem_limit_bytes=VMEM_LIMIT),
        cost_estimate=pl.CostEstimate(flops=15 * 10**9, bytes_accessed=25 * 10**6, transcendentals=3 * 10**6),
        name="attention_backward",
    )(tokens, cotangent, hidden, packed, mixed, lse, part_own, part_other, wqkv, wout, par)

    owed = jnp.concatenate(
        [
            gqkv.reshape(groups, part, 3, span, wide).transpose(0, 3, 1, 2, 4).reshape(groups * span, -1),
            gout.reshape(span, wide, groups, part).transpose(2, 0, 1, 3).reshape(groups * span, -1),
            jnp.repeat(gpar[:4].reshape(4, groups, part).transpose(1, 0, 2).reshape(groups, -1), span, axis=0),
        ],
        1,
    )
    owed = jnp.pad(owed, ((0, 0), (0, rounded - length)))
    mine = lax.psum_scatter(owed, ALL, scatter_dimension=0, tiled=False)
    vectors = mine[sizes[0] + sizes[1] : length].reshape(4, part)
    return (
        output,
        grad_tokens,
        mine[: sizes[0]].reshape(part, 3, wide),
        mine[sizes[0] : sizes[0] + sizes[1]].reshape(wide, part),
        vectors[0],
        vectors[1],
        vectors[2],
        vectors[3],
        grad_shard[:, 0].transpose(0, 2, 1),
        grad_shard[:, 1],
    )


def solution(mesh):
    groups, span = mesh.devices.shape
    split = Mesh(mesh.devices.reshape(groups // 2, 2, span), ALL)
    return jax.shard_map(
        on_device,
        mesh=split,
        in_specs=(
            P(ALL, None),
            P(DP, None, "tensor"),
            P("tensor", DP),
            P(DP),
            P(DP),
            P(DP),
            P(DP),
            P(None, None, ALL),
            P(None, ALL, None),
            P(DP, None),
            P(DP, None),
            P(ALL, None),
        ),
        out_specs=(
            P(ALL, None),
            P(ALL, None),
            P(DP, None, "tensor"),
            P("tensor", DP),
            P(DP),
            P(DP),
            P(DP),
            P(DP),
            P(None, None, ALL),
            P(None, ALL, None),
        ),
        check_vma=False,
    )
```

time: 1490 us -> 716 us (0.48); the launches traced: 1470 us -> 716 us
  other arithmetic: 291 us -> 6.67 us
  matrix products: 279 us -> 0.19 us
  local copies, waits for them, and re-layouts: 333 us -> 57.3 us
  blocking collectives: 269 us -> 0 us
  Pallas kernels: 0 us -> 186 us
  waiting for transfers between devices: 273 us -> 451 us
    dot_general x89 -> x1, matrix products: 279 us -> 0.19 us  [route(): rank = jnp.einsum('ber,rs->bes', named, earlier, preferred_element_type=F32)]
    scatter-add x16 -> x0, other arithmetic: 250 us -> none  [the longest x8 126 us: per_expert(): back_sum = back_sum.at[slot_rows].add(grad_loaded)]
    unnamed x5 -> x0, blocking collectives: 223 us -> none
    pallas_call x0 -> x3, Pallas kernels: none -> 186 us  [the longest x1 119 us: on_device(): pl.pallas_call(experts, out_shape=(whole((padded, 2 * width), BF16), whol...]
    unnamed x14 -> x5, waiting for transfers between devices: 3.94 us -> 136 us
    gather x16 -> x0, local copies, waits for them, and re-layouts: 89.9 us -> none  [the longest x8 53 us: per_expert(): loaded = padded[slot_rows]]
    scatter x2 -> x0, local copies, waits for them, and re-layouts: 73.8 us -> none  [the longest x1 36.9 us: expert_pass(): owners = jnp.full((number * CAP,), row_count, jnp.int32).at[position].set...]
    unnamed x97 -> x24, local copies, waits for them, and re-layouts: 65.6 us -> 6.78 us
  transfers between devices with their start and end apart: 14 -> 8, of which waited for: 6 -> 6; matrix products, arithmetic and copies ran while one was open for 23% -> 4% of each run, Pallas kernels for 0% -> 3%
where the time goes in v1:
time: 716 us
  waiting for transfers between devices  451 us (63%)
  Pallas kernels  186 us (26%)
  local copies, waits for them, and re-layouts  57.3 us (8%)
  between operations  14.1 us (2%)
    reduce_scatter x1, waiting for transfers between devices, on_device(): lax.psum_scatter(grads, RING, scatter_dimension=0, tiled=False).astype(F32)  171 us
    unnamed x5, waiting for transfers between devices  136 us
    pallas_call x1, Pallas kernels, on_device(): pl.pallas_call(experts, out_shape=(whole((padded, 2 * width), BF16), whol...  119 us
    all_gather x1, waiting for transfers between devices, on_device(): weights = lax.all_gather(shard, RING, axis=0, tiled=False)  82.5 us
    all_gather x1, waiting for transfers between devices, on_device(): lax.all_gather(jnp.pad(small, (0, rounded - length)), ALL, axis=0, tiled=...  52.7 us
    pallas_call x1, Pallas kernels, on_device(): pl.pallas_call(attention_backward, out_shape=(whole((rows, width), BF16),...  43.2 us
    pallas_call x1, Pallas kernels, on_device(): pl.pallas_call(attention_forward, out_shape=(whole((padded, width), BF16)...  23.4 us
  transfers between devices with their start and end apart: 8, of which 6 were waited for; matrix products, arithmetic and copies ran while one was open for 4% of the time, Pallas kernels for 3%

profile of v1, /device:TPU:0, one launch (start us, length us, event | category | flops | bytes accessed | tf_op | source)
XLA Modules:
  0.0 715.7 jit_solution(1879665709699808412)
XLA Ops:
  7.3 0.9 copy.72
  8.3 0.8 copy.73
  9.2 2.8 concatenate.12
  12.0 0.6 pad.24
  12.7 1.9 pad_maximum_fusion
  14.7 1.3 pad.28.cown
  16.0 0.5 collective-permute-start.2
  17.1 52.7 %all-gather.5.cloned.1.call-done = bf16[622592]{0:T(1024)(128)(2,1)} async-done(((bf16[19456]{0:T(1024)(128)(2,1)}), bf16[622592]{0:T(1024)(128)(2,1)}) %all-gather.5.cloned.1.call-update) | async-done | bytes 1245200 | tf_op jit(solution)/shard_map/all_gather | solution.py:400
  69.8 1.6 reshape.142
  71.5 1.0 copy-done.3
  72.5 1.8 reshape.125
  74.3 1.8 copy.74
  76.2 1.7 reshape.126.wqkv
  77.9 2.5 reshape.127
  80.4 0.9 copy.75
  81.5 0.9 copy.77.wout
  82.4 0.3 reshape.129
  82.8 0.7 reshape.139.par
  83.5 23.4 %attention_forward.1 = (bf16[1984,384]{1,0:T(8,128)(2,1)}, f32[1984,384]{1,0:T(8,128)}, bf16[1984,1152]{1,0:T(8,128)(2,1)}, bf16[1984,384]{1,0:T(8,128)(2,1)}, f32[1984,128]{1,0:T(8,128)}) custom-call(bf16[1970,384]{1,0:T(8,128)(2,1)} %tok.3, bf16[384,1152]{1,0:T(8,128)(2,1)} %reshape.126.wqkv, bf16[384,384]{1,0:T(8,128)(2,1)} %copy.77.wout, ...), custom_call_target="tpu_custom_call" | custom-call | flops 6000000000 | bytes 14000000 | tf_op jit(solution)/shard_map/attention_forward/pallas_call | solution.py:435
  107.8 0.4 collective-permute-start
  108.2 2.4 collective-permute-done.tsib
  110.6 0.6 convert_element_type.46.cnt
  111.2 82.5 %all-gather.7.cloned.1.call-done = bf16[128,2,48,384]{3,2,0,1:T(8,128)(2,1)} async-done(((bf16[8,2,48,384]{3,2,0,1:T(8,128)(2,1)}), bf16[128,2,48,384]{3,2,0,1:T(8,128)(2,1)}) %all-gather.7.cloned.1.call-update) | async-done | bytes 9437200 | tf_op jit(solution)/shard_map/all_gather | solution.py:422
  193.8 8.4 %copy.80 = bf16[128,2,48,384]{3,2,1,0:T(8,128)(2,1)} copy(bf16[128,2,48,384]{3,2,0,1:T(8,128)(2,1)} %all-gather.7.cloned.1.call-done) | data formatting | bytes 18874368 | tf_op jit(solution)/shard_map/all_gather | solution.py:422
  202.1 1.1 copy-done.9
  203.3 119.0 %experts.1 = (bf16[1984,768]{1,0:T(8,128)(2,1)}, bf16[1984,768]{1,0:T(8,128)(2,1)}, bf16[16,8,2,48,384]{4,3,2,1,0:T(8,128)(2,1)}) custom-call(s32[64]{0:T(128)} %convert_element_type.46.cnt, bf16[1984,384]{1,0:T(8,128)(2,1)} %get-tuple-element.27.rown, bf16[1984,384]{1,0:T(8,128)(2,1)} %copy-done.9, bf16[1984,384]{1,0:T(8,128)(2,1)} %pad.28.cown, ...), custom_call_target="tpu_custom_call" | custom-call | flops 49999998976 | bytes 40000000 | tf_op jit(solution)/shard_map/experts/pallas_call | solution.py:466
  322.3 5.7 collective-permute-done.3.other
  328.0 1.6 copy-done.8
  329.6 43.2 %attention_backward.1 = (bf16[1970,384]{1,0:T(8,128)(2,1)}, f32[1970,384]{1,0:T(8,128)}, f32[384,1152]{1,0:T(8,128)}, f32[384,384]{1,0:T(8,128)}, f32[8,384]{1,0:T(8,128)}) custom-call(bf16[1970,384]{1,0:T(8,128)(2,1)} %tok.3, bf16[1970,384]{1,0:T(8,128)(2,1)} %cot.1, f32[1984,384]{1,0:T(8,128)} %get-tuple-element.23.hidden_r, ...), custom_call_target="tpu_custom_call" | custom-call | flops 15000000512 | bytes 25000000 | tf_op jit(solution)/shard_map/attention_backward/pallas_call | solution.py:502
  372.8 0.7 slice.85
  373.7 1.3 copy.83
  375.0 1.4 reshape.132
  376.5 2.0 copy.84
  378.5 3.0 reshape.133
  381.5 4.4 reshape.130
  385.9 2.5 copy.92
  388.4 2.9 reshape.131
  391.3 3.3 select_maximum_fusion
  394.7 0.5 reduce-scatter.2.cloned.1.call-update
  395.2 135.7 %all-reduce.9.cloned.1.call-done = f32[32,19456]{1,0:T(8,128)} async-done(((f32[32,19456]{1,0:T(8,128)}), f32[32,19456]{1,0:T(8,128)}) %all-reduce.9.cloned.1.call-update) | async-done | bytes 2490384
  531.0 1.2 dynamic-slice_reduce_fusion
  532.2 0.6 copy.86
  532.9 1.0 dynamic-slice_reduce_fusion.1
  534.0 0.7 copy.87
  534.7 1.4 dynamic-slice_bitcast_fusion.2
  536.1 170.8 %reduce-scatter.2.cloned.1.call-done = bf16[1,8,2,48,384]{4,3,2,1,0:T(8,128)(2,1)} async-done(((bf16[16,8,2,48,384]{4,3,2,1,0:T(8,128)(2,1)}), bf16[1,8,2,48,384]{4,3,2,1,0:T(8,128)(2,1)}) %reduce-scatter.2.cloned.1.call-update) | async-done | bytes 589840 | tf_op jit(solution)/shard_map/reduce_scatter | solution.py:500
  706.9 1.1 bitcast_convert_fusion
  708.1 1.1 slice_bitcast_fusion
  (66 shorter events, 2.6 us)
Async XLA Ops:
  7.2 9.3 %copy-start = (s32[3940,2]{0,1:T(2,128)S(1)}, s32[3940,2]{0,1:T(2,128)}, u32[]{:S(2)}) copy-start(s32[3940,2]{0,1:T(2,128)} %param.21) | copy-start | bytes 94564
  7.2 7.5 %copy-start.4 = (bf16[1970,384]{1,0:T(8,128)(2,1)S(1)}, bf16[1970,384]{1,0:T(8,128)(2,1)}, u32[]{:S(2)}) copy-start(bf16[1970,384]{1,0:T(8,128)(2,1)} %cot.1) | copy-start | bytes 4538884
  7.2 62.6 %all-gather.5.cloned.1.call-start = ((), (), s32[]{:S(2)}) async-start(), calls=%async_computation.2 | async-start | bytes 1284096 | tf_op jit(solution)/shard_map/all_gather | solution.py:400
  12.6 4.1 copy-start.6
  12.6 181.1 %all-gather.7.cloned.1.call-start = ((), (), s32[]{:S(2)}) async-start(), calls=%async_computation.3 | async-start | bytes 10027008 | tf_op jit(solution)/shard_map/all_gather | solution.py:422
  14.6 516.3 %all-reduce.9.cloned.1.call-start = ((), (), s32[]{:S(2)}) async-start(), calls=%async_computation.4 | async-start | bytes 4980736
  16.0 186.1 %collective-permute-start.2 = (bf16[1984,384]{1,0:T(8,128)(2,1)}, bf16[1984,384]{1,0:T(8,128)(2,1)}, u32[]{:S(2)}, u32[]{:S(2)}) collective-permute-start(bf16[1984,384]{1,0:T(8,128)(2,1)} %pad.28.cown), channel_id=1, source_target_pairs={{0,2},{2,0},{1,3},{3,1},{4,6},{6,4},{5,7},{7,5},{8,10},{10,8},{9,1... | collective-permute-start | bytes 4571144 | tf_op jit(solution)/shard_map/ppermute | solution.py:433
  71.4 1.0 copy-start.3
  74.3 3.5 slice-start
  77.9 4.5 copy-start.2
  107.0 95.2 %collective-permute-start.1 = (bf16[1984,384]{1,0:T(8,128)(2,1)}, bf16[1984,384]{1,0:T(8,128)(2,1)S(1)}, u32[]{:S(2)}, u32[]{:S(2)}) collective-permute-start(bf16[1984,384]{1,0:T(8,128)(2,1)} %get-tuple-element.27.rown), channel_id=1, source_target_pairs={{0,2},{2,0},{1,3},{3,1},{4,6},{6,4},{5,7},{7,5},{8,10},{10,8},{9,1... | collective-permute-start | bytes 4571144 | tf_op jit(solution)/shard_map/ppermute | solution.py:451
  107.8 94.3 %copy-start.5 = (f32[4,8,496]{2,1,0:T(8,128)}, f32[4,8,496]{2,1,0:T(8,128)S(1)}, u32[]{:S(2)}) copy-start(f32[4,8,496]{2,1,0:T(8,128)S(1)} %concatenate.13.town) | copy-start | bytes 190468
  107.8 2.8 collective-permute-start
  110.6 91.5 %copy-start.7 = (f32[4,8,496]{2,1,0:T(8,128)}, f32[4,8,496]{2,1,0:T(8,128)S(1)}, u32[]{:S(2)}) copy-start(f32[4,8,496]{2,1,0:T(8,128)S(1)} %collective-permute-done.tsib) | copy-start | bytes 190468
  202.1 1.1 copy-start.9
  322.3 5.7 collective-permute-start.3
  328.0 1.6 copy-start.8
  394.6 312.3 %reduce-scatter.2.cloned.1.call-start = ((), (), s32[]{:S(2)}) async-start(), calls=%async_computation.1 | async-start | bytes 10027008 | tf_op jit(solution)/shard_map/reduce_scatter | solution.py:500
  395.2 314.0 %copy-start.1 = (s32[3940,2]{0,1:T(2,128)S(1)}, s32[3940,2]{0,1:T(2,128)}, u32[]{:S(2)}) copy-start(s32[3940,2]{0,1:T(2,128)} %param.21) | copy-start | bytes 94564
Sparse Core Ops, SparseCore 0:
  12.7 57.0 all-gather.4
  73.0 120.6 all-gather.6
  394.7 136.1 all-reduce.8
  536.5 170.4 reduce-scatter.1
